TPU v7x, 256 devices: a 8x8x2 block of a 8x8x16 slice. The times are simulated.
256 devices in a mesh: rep: 2 (over z), tp: 16 (over y, core), sub: 8 (over x).
Axes of the slice: x: 8, y: 8, z: 2, core: 2. Of those that a mesh axis runs over, the one named last changes fastest.
The devices are a block of a 8x8x16 slice.
Arguments:
- acts: bfloat16 [2048, 16384], P(('rep', 'tp'), 'sub'), parts along dimension 0, may hold values from -6 to 6
- q_src: bfloat16 [32768, 16384], P(('rep', 'sub'), 'tp'), parts along dimension 0, may hold values from -0.046875 to 0.046875
- kv_src: bfloat16 [32768, 2048], P(('rep', 'sub'), 'tp'), parts along dimension 0, may hold values from -0.046875 to 0.046875
- q_src_heads: int32 [128], replicated, may hold values from 0 to 127, as said below
- q_tgt_heads: int32 [128], replicated, may hold values from 0 to 127, as said below
- kv_tgt_heads: int32 [16], replicated, may hold values from 0 to 7, as said below
Outputs:
- q_new: bfloat16 [32768, 16384], P(('rep', 'sub'), 'tp'), parts along dimension 0
- kv_new: bfloat16 [32768, 4096], P(('rep', 'sub'), 'tp'), parts along dimension 0
- qkv: bfloat16 [2048, 20480], P(('rep', 'sub'), 'tp'), parts along dimension 0
There are 2 independent parts, one for each index of `rep`. A program takes and returns all parts, laid end to end along the dimension named above; an argument that names none is the same for every part. Nothing has to cross between parts.
Inputs may be any that keep to these rules, and one draw needn't show every extreme that they name: q_src_heads and q_tgt_heads are permutations. Source block t is entries t * 8 to (t + 1) * 8 - 1 of q_src_heads, target block j the same entries of q_tgt_heads. With s = 4, source block t shares exactly 2 heads with target block (t + min(1, s - 1)) mod 16 and with each target block (t + k * s) mod 16 for k from 1 to 3, and none with any other. `q_tgt_heads`: see q_src_heads. `kv_tgt_heads`: every key-value head appears exactly twice.
All inputs are finite; a program needn't handle non-finite values.
Results may differ from a plain program's by a relative error of at most 0.001.
Values may be sent and summed in bfloat16 or wider, within the bound.
A program may use at most 128 MiB of HBM per device.

v0:
```python
import jax
import jax.numpy as jnp
from jax import lax
from jax.sharding import PartitionSpec as P

HD = 128


def from_behind(block, axis, distance):
    devices = range(lax.axis_size(axis))
    route = [((i - distance) % len(devices), i) for i in devices]
    return lax.ppermute(block, axis, route)


def per_device(acts, q_src, kv_src, q_src_heads, q_tgt_heads, kv_tgt_heads):
    tp_count = lax.axis_size("tp")
    my_index = lax.axis_index("tp")
    row_count = q_src.shape[0]
    q_local = q_src.shape[1] // HD
    capacity = max(2, q_local // tp_count)
    select_count = q_local // capacity
    stride = tp_count // select_count
    head_count = q_src_heads.shape[0]
    head_ids = jnp.arange(head_count, dtype=jnp.int32)
    matches = (q_src_heads[None, :] == q_tgt_heads[:, None]).astype(jnp.int32)
    target_pos = jnp.sum(matches * head_ids[:, None], axis=0)
    slot_of = jnp.sum(matches * head_ids[None, :], axis=1)
    target_dev = target_pos // q_local
    source_dev = head_ids // q_local
    earlier = (
        (source_dev[:, None] == source_dev[None, :])
        & (target_dev[:, None] == target_dev[None, :])
        & (head_ids[None, :] < head_ids[:, None])
    )
    slot_rank = jnp.sum(earlier.astype(jnp.int32), axis=1)
    own_target = lax.dynamic_slice_in_dim(target_dev, my_index * q_local, q_local)
    own_rank = lax.dynamic_slice_in_dim(slot_rank, my_index * q_local, q_local)
    buffer_ids = jnp.arange(tp_count * capacity, dtype=jnp.int32)
    slot_hit = ((own_target * capacity + own_rank)[None, :] == buffer_ids[:, None]).astype(
        jnp.int32
    )
    pick_slot = jnp.sum(slot_hit * jnp.arange(q_local, dtype=jnp.int32)[None, :], axis=1)
    my_slots = lax.dynamic_slice_in_dim(slot_of, my_index * q_local, q_local)
    pick_table = pick_slot.reshape(tp_count, capacity)
    q_three = q_src.reshape(row_count, q_local, HD)
    pieces = []
    for step_number in range(select_count):
        if step_number == 0:
            distance = min(1, stride - 1)
        else:
            distance = step_number * stride
        target_block = (my_index + distance) % tp_count
        chosen_slots = lax.dynamic_index_in_dim(pick_table, target_block, 0, keepdims=False)
        outgoing_piece = jnp.take(q_three, chosen_slots, axis=1)
        outgoing_piece = from_behind(outgoing_piece, "tp", distance)
        pieces.append(outgoing_piece)
    stacked = jnp.concatenate(pieces, axis=1)
    source_block = my_slots // q_local
    offset = (my_index - source_block) % tp_count
    shift_rank = jnp.where(offset % stride == 0, offset // stride, 0)
    compact_ids = shift_rank * capacity + slot_rank[my_slots]
    q_new = jnp.take(stacked, compact_ids, axis=1).reshape(row_count, q_local * HD)
    kv_slots = kv_tgt_heads.shape[0] // tp_count
    kv_whole = lax.all_gather(kv_src, "tp", axis=1, tiled=True)
    own_kv = lax.dynamic_slice_in_dim(kv_tgt_heads, my_index * kv_slots, kv_slots)
    kv_three = kv_whole.reshape(row_count, kv_whole.shape[1] // (2 * HD), 2 * HD)
    kv_new = jnp.take(kv_three, own_kv, axis=1).reshape(row_count, kv_slots * 2 * HD)
    gathered = lax.all_gather(acts, "tp", axis=0, tiled=True)
    joined_cols = jnp.concatenate([q_new, kv_new], axis=1)
    qkv = lax.psum_scatter(
        jnp.dot(gathered, joined_cols, preferred_element_type=jnp.float32),
        "sub",
        scatter_dimension=0,
        tiled=True,
    ).astype(jnp.bfloat16)
    return (q_new, kv_new, qkv)


def solution(mesh):
    in_specs = (
        P(("rep", "tp"), "sub"),
        P(("rep", "sub"), "tp"),
        P(("rep", "sub"), "tp"),
        P(),
        P(),
        P(),
    )
    out_specs = (P(("rep", "sub"), "tp"), P(("rep", "sub"), "tp"), P(("rep", "sub"), "tp"))
    return jax.shard_map(
        per_device, mesh=mesh, in_specs=in_specs, out_specs=out_specs, check_vma=False
    )
```

profile of v0, /device:TPU:513, one launch (start us, length us, event | category | flops | bytes accessed | tf_op | source)
XLA Modules:
  0.0 309.0 jit_solution(1556637233331579625)
XLA Ops:
  7.2 2.0 copy.30
  11.6 6.4 %copy.24 = bf16[2048,1024]{0,1:T(8,128)(2,1)} copy(bf16[2048,1024]{1,0:T(8,128)(2,1)} %param.9) | data formatting | bytes 8388608 | tf_op args[1]
  18.0 6.5 %copy.25 = bf16[2048,8,128]{2,0,1:T(8,128)(2,1)} copy(bf16[2048,8,128]{0,2,1:T(8,128)(2,1)} %bitcast.43) | data formatting | bytes 8388608 | tf_op jit(solution)/shard_map/reshape | solution.py:45
  24.5 2.9 gather_fusion.2
  27.6 3.9 %collective-permute-start = (bf16[2048,2,128]{2,0,1:T(8,128)(2,1)S(1)}, bf16[2048,2,128]{2,0,1:T(8,128)(2,1)}, u32[]{:S(2)}, u32[]{:S(2)}) collective-permute-start(bf16[2048,2,128]{2,0,1:T(8,128)(2,1)S(1)} %select_bitcast_fusion.3), channel_id=1, source_target_pairs={{120,0},{0,8},{8,16},{16,24},{24,32},{32,40},{40,48},{48,56},{56,6... | collective-permute-start | bytes 3145736 | tf_op jit(solution)/shard_map/ppermute | solution.py:12
  31.5 2.9 gather_fusion.3
  34.6 4.8 %collective-permute-start.1 = (bf16[2048,2,128]{2,0,1:T(8,128)(2,1)S(1)}, bf16[2048,2,128]{2,0,1:T(8,128)(2,1)}, u32[]{:S(2)}, u32[]{:S(2)}) collective-permute-start(bf16[2048,2,128]{2,0,1:T(8,128)(2,1)S(1)} %select_bitcast_fusion.2), channel_id=1, source_target_pairs={{96,0},{104,8},{112,16},{120,24},{0,32},{8,40},{16,48},{24,56},{32... | collective-permute-start | bytes 3145736 | tf_op jit(solution)/shard_map/ppermute | solution.py:12
  39.4 2.9 gather_fusion.4
  42.4 1.1 select_bitcast_fusion.1
  43.5 7.6 %collective-permute-start.2 = (bf16[2048,2,128]{2,0,1:T(8,128)(2,1)}, bf16[2048,2,128]{2,0,1:T(8,128)(2,1)}, u32[]{:S(2)}, u32[]{:S(2)}) collective-permute-start(bf16[2048,2,128]{2,0,1:T(8,128)(2,1)} %select_bitcast_fusion.1), channel_id=1, source_target_pairs={{64,0},{72,8},{80,16},{88,24},{96,32},{104,40},{112,48},{120,56},{... | collective-permute-start | bytes 3145736 | tf_op jit(solution)/shard_map/ppermute | solution.py:12
  51.2 3.0 gather_fusion.5
  54.2 1.1 select_bitcast_fusion
  59.4 103.9 %collective-permute-done.1 = bf16[2048,2,128]{2,0,1:T(8,128)(2,1)} collective-permute-done((bf16[2048,2,128]{2,0,1:T(8,128)(2,1)S(1)}, bf16[2048,2,128]{2,0,1:T(8,128)(2,1)}, u32[]{:S(2)}, u32[]{:S(2)}) %collective-permute-start.1) | collective-permute-done | bytes 1048608 | tf_op jit(solution)/shard_map/ppermute | solution.py:12
  163.3 19.3 %collective-permute-done.2 = bf16[2048,2,128]{2,0,1:T(8,128)(2,1)} collective-permute-done((bf16[2048,2,128]{2,0,1:T(8,128)(2,1)}, bf16[2048,2,128]{2,0,1:T(8,128)(2,1)}, u32[]{:S(2)}, u32[]{:S(2)}) %collective-permute-start.2) | collective-permute-done | bytes 1048608 | tf_op jit(solution)/shard_map/ppermute | solution.py:12
  182.6 3.6 %pad_maximum_fusion = bf16[2048,8,128]{2,0,1:T(8,128)(2,1)} fusion(bf16[2048,2,128]{2,0,1:T(8,128)(2,1)S(1)} %collective-permute-done.3, bf16[2048,2,128]{2,0,1:T(8,128)(2,1)} %collective-permute-done.2, bf16[2048,2,128]{2,0,1:T(8,128)(2,1)} %collective-permute-done.1, bf16[2048,2,128]{2,0,1:T(8,128)(2,1)} %collective-permute-done), kind=kLoop, calls=%fused_computation.11 | loop fusion | flops 6291456 | bytes 8388608 | tf_op jit(solution)/shard_map/concatenate | solution.py:57
  186.2 5.2 %gather_fusion.1 = bf16[8,2048,128]{2,1,0:T(8,128)(2,1)} fusion(bf16[2048,8,128]{2,0,1:T(8,128)(2,1)} %pad_maximum_fusion, s32[1024]{0:T(1024)S(1)} %pad_clamp_fusion), kind=kCustom, calls=%fused_computation.5 | custom fusion | bytes 8388640 | tf_op jit(solution)/shard_map/jit(_take)/gather | solution.py:62
  191.4 6.4 %copy.29 = bf16[2048,8,128]{0,2,1:T(8,128)(2,1)} copy(bf16[2048,8,128]{2,0,1:T(8,128)(2,1)} %bitcast.42) | data formatting | bytes 8388608 | tf_op jit(solution)/shard_map/jit(_take)/gather | solution.py:62
  197.8 4.6 %bitcast_select_fusion = bf16[2048,1024]{0,1:T(8,128)(2,1)} fusion(bf16[2048,8,128]{0,2,1:T(8,128)(2,1)} %copy.29, pred[1024]{0:T(1024)(128)(4,1)S(1)} %broadcast_bitcast_fusion), kind=kLoop, calls=%fused_computation.12 | loop fusion | flops 2097152 | bytes 8389632 | tf_op jit(solution)/shard_map/jit(_take)/select_n | solution.py:62
  202.4 1.4 select_bitcast_fusion.4
  203.8 21.9 %all-gather.5.cloned.1.call-done = bf16[1024,2048]{1,0:T(8,128)(2,1)} async-done(((bf16[64,2048]{1,0:T(8,128)(2,1)}), bf16[1024,2048]{1,0:T(8,128)(2,1)}) %all-gather.5.cloned.1.call-update) | async-done | bytes 4194320 | tf_op jit(solution)/shard_map/all_gather | solution.py:68
  225.7 10.2 %fusion.4 = f32[1024,1280]{0,1:T(8,128)} fusion(bf16[1024,2048]{1,0:T(8,128)(2,1)} %all-gather.5.cloned.1.call-done, bf16[2048,256]{0,1:T(8,128)(2,1)S(1)} %select_bitcast_fusion.4, bf16[2048,1024]{0,1:T(8,128)(2,1)} %bitcast_select_fusion), kind=kOutput, calls=%fused_computation.10 | convolution fusion | flops 5379194880 | bytes 14680064 | tf_op jit(solution)/shard_map/dot_general | solution.py:71
  236.0 6.4 %copy.31 = bf16[2048,1024]{1,0:T(8,128)(2,1)} copy(bf16[2048,1024]{0,1:T(8,128)(2,1)} %bitcast_select_fusion) | data formatting | bytes 8388608
  242.4 1.3 copy.32
  243.7 56.8 %reduce-scatter.2.cloned.1.call-done = f32[128,1280]{0,1:T(8,128)} async-done(((f32[1024,1280]{0,1:T(8,128)}), f32[128,1280]{0,1:T(8,128)}) %reduce-scatter.2.cloned.1.call-update) | async-done | bytes 655376 | tf_op jit(solution)/shard_map/reduce_scatter | solution.py:70
  (34 shorter events, 6.8 us)
Async XLA Ops:
  7.2 195.3 %all-gather.3.cloned.1.call-start = ((), (), s32[]{:S(2)}) async-start(), calls=%async_computation.1 | async-start | bytes 8912896 | tf_op jit(solution)/shard_map/all_gather | solution.py:64
  9.3 216.3 %all-gather.5.cloned.1.call-start = ((), (), s32[]{:S(2)}) async-start(), calls=%async_computation.2 | async-start | bytes 4456448 | tf_op jit(solution)/shard_map/all_gather | solution.py:68
  10.2 290.3 %reduce-scatter.2.cloned.1.call-start = ((), (), s32[]{:S(2)}) async-start(), calls=%async_computation.3 | async-start | bytes 5898240 | tf_op jit(solution)/shard_map/reduce_scatter | solution.py:70
  27.6 31.8 %collective-permute-start = (bf16[2048,2,128]{2,0,1:T(8,128)(2,1)S(1)}, bf16[2048,2,128]{2,0,1:T(8,128)(2,1)}, u32[]{:S(2)}, u32[]{:S(2)}) collective-permute-start(bf16[2048,2,128]{2,0,1:T(8,128)(2,1)S(1)} %select_bitcast_fusion.3), channel_id=1, source_target_pairs={{120,0},{0,8},{8,16},{16,24},{24,32},{32,40},{40,48},{48,56},{56,6... | collective-permute-start | bytes 3145736 | tf_op jit(solution)/shard_map/ppermute | solution.py:12
  34.6 128.7 %collective-permute-start.1 = (bf16[2048,2,128]{2,0,1:T(8,128)(2,1)S(1)}, bf16[2048,2,128]{2,0,1:T(8,128)(2,1)}, u32[]{:S(2)}, u32[]{:S(2)}) collective-permute-start(bf16[2048,2,128]{2,0,1:T(8,128)(2,1)S(1)} %select_bitcast_fusion.2), channel_id=1, source_target_pairs={{96,0},{104,8},{112,16},{120,24},{0,32},{8,40},{16,48},{24,56},{32... | collective-permute-start | bytes 3145736 | tf_op jit(solution)/shard_map/ppermute | solution.py:12
  39.4 17.2 %copy-start = (s32[16]{0:T(128)S(1)}, s32[16]{0:T(128)}, u32[]{:S(2)}) copy-start(s32[16]{0:T(128)} %param.13) | copy-start | bytes 196
  43.5 139.0 %collective-permute-start.2 = (bf16[2048,2,128]{2,0,1:T(8,128)(2,1)}, bf16[2048,2,128]{2,0,1:T(8,128)(2,1)}, u32[]{:S(2)}, u32[]{:S(2)}) collective-permute-start(bf16[2048,2,128]{2,0,1:T(8,128)(2,1)} %select_bitcast_fusion.1), channel_id=1, source_target_pairs={{64,0},{72,8},{80,16},{88,24},{96,32},{104,40},{112,48},{120,56},{... | collective-permute-start | bytes 3145736 | tf_op jit(solution)/shard_map/ppermute | solution.py:12
  55.4 127.2 %collective-permute-start.3 = (bf16[2048,2,128]{2,0,1:T(8,128)(2,1)}, bf16[2048,2,128]{2,0,1:T(8,128)(2,1)S(1)}, u32[]{:S(2)}, u32[]{:S(2)}) collective-permute-start(bf16[2048,2,128]{2,0,1:T(8,128)(2,1)} %select_bitcast_fusion), channel_id=1, source_target_pairs={{32,0},{40,8},{48,16},{56,24},{64,32},{72,40},{80,48},{88,56},{96,... | collective-permute-start | bytes 3145736 | tf_op jit(solution)/shard_map/ppermute | solution.py:12
Sparse Core Ops, SparseCore 0:
  9.9 152.4 all-gather.2
  164.2 61.4 all-gather.4
  236.1 64.2 reduce-scatter.1
where the time goes:
time: 310 us; the launch traced here: 309 us
  waiting for transfers between devices  203 us (65%)
  local copies, waits for them, and re-layouts  48.4 us (16%)
  starting transfers between devices  17.1 us (6%)
  between operations  15.9 us (5%)
  other arithmetic  14.7 us (5%)
  matrix products  10.2 us (3%)
    ppermute x4, waiting for transfers between devices, from_behind(): return lax.ppermute(block, axis, route)  123 us
    reduce_scatter x1, waiting for transfers between devices, per_device(): lax.psum_scatter(jnp.dot(gathered, joined_cols, preferred_element_type=jn...  56.8 us
    all_gather x1, waiting for transfers between devices, per_device(): gathered = lax.all_gather(acts, 'tp', axis=0, tiled=True)  21.9 us
    unnamed x7, local copies, waits for them, and re-layouts  17.1 us
    ppermute x4, starting transfers between devices, from_behind(): return lax.ppermute(block, axis, route)  16.9 us
    gather x4, local copies, waits for them, and re-layouts, per_device(): outgoing_piece = jnp.take(q_three, chosen_slots, axis=1)  11.8 us
    gather x2, local copies, waits for them, and re-layouts, per_device(): jnp.take(stacked, compact_ids, axis=1).reshape(row_count, q_local * HD)  11.6 us
    dot_general x1, matrix products, per_device(): jnp.dot(gathered, joined_cols, preferred_element_type=jnp.float32)  10.2 us
  transfers between devices with their start and end apart: 7, of which 4 were waited for; matrix products, arithmetic and copies ran while one was open for 19% of the time, Pallas kernels for 0%

commit v1 on v0

v1 whole, which is shorter than its diff:
```python
import functools

import jax
import jax.numpy as jnp
from jax import lax
from jax.experimental import pallas as pl
from jax.experimental.pallas import tpu as pltpu
from jax.sharding import PartitionSpec as P

HD = 128
F32, BF16 = jnp.float32, jnp.bfloat16
FILL = 16


def distances(tp, heads):
    capacity = max(2, heads // tp)
    select = heads // capacity
    stride = tp // select
    return [min(1, stride - 1)] + [k * stride for k in range(1, select)], capacity, stride


def mul(index, size):
    return pl.multiple_of(index * size, size)


def exchange(tp, subs, sel_ref, kvt_ref, acts_ref, q_ref, kv_ref, qraw, kvraw, sraw, kvres,
             acts, qv, sendq, kvbuf, kvsend, part, rsbuf, res, ssel, ld, asend, arecv, apsend, aprecv,
             ksend, krecv, kpsend, kprecv, qsend, qrecv, fsend, frecv, rsend, rrecv, ss_send, ss_recv):
    t, x = lax.axis_index("tp"), lax.axis_index("sub")
    core, y = lax.rem(t, 2), t // 2
    ring = tp // 2
    full = ring // 2 - 1
    toks, rows = acts_ref.shape[0], q_ref.shape[0]
    heads = q_ref.shape[1] // HD
    dist, cap, _ = distances(tp, heads)
    mate = t + 1 - 2 * core

    def at(d):
        return lax.rem(t + d + tp, tp)

    def remote(src, dst, send, recv, **where):
        copy = pltpu.make_async_remote_copy(
            src_ref=src, dst_ref=dst, send_sem=send, recv_sem=recv, device_id=where)
        copy.start()
        return copy

    def rows_of(index, first=0, count=toks):
        return acts.at[pl.ds(mul(index, toks) + first, count)]

    loads = [
        pltpu.make_async_copy(acts_ref, rows_of(t), ld.at[0]),
        pltpu.make_async_copy(kv_ref, kvbuf.at[y], ld.at[1]),
    ] + [pltpu.make_async_copy(q_ref.at[:, pl.ds(i * HD, HD)], qv.at[i], ld.at[2 + i]) for i in range(heads)]
    for copy in loads:
        copy.start()
    barrier = pltpu.get_barrier_semaphore()
    peers = {1, tp - 1, 2, tp - 2} | set(dist) | {tp - d for d in dist}
    for d in sorted(peers):
        pl.semaphore_signal(barrier, inc=1, device_id={"tp": at(d)})
    for d in (1, subs - 1):
        pl.semaphore_signal(barrier, inc=1, device_id={"sub": lax.rem(x + d, subs)})
    for copy in loads:
        copy.wait()
    for i in range(heads):
        sendq[i] = qv[sel_ref[i]]
    pl.semaphore_wait(barrier, len(peers) + 2)

    sent = []
    for d in (0, 1):
        sent.append(remote(rows_of(t), rows_of(t), asend.at[d, 0], arecv.at[d, 0], tp=at(2 - 4 * d)))
    sent.append(remote(rows_of(t), rows_of(t), apsend.at[0], aprecv.at[0], tp=mate))
    fills = []
    far = len(dist) // 2
    per_head = FILL // cap
    span = rows // per_head

    def fill(count):
        for _ in range(count):
            i = len(fills)
            if i == FILL:
                return
            head, piece = far * cap + i % cap, i // cap
            cut = pl.ds(piece * span, span)
            fills.append(remote(sendq.at[head, cut], qraw.at[head, cut], fsend.at[i], frecv.at[i], tp=at(dist[far])))

    fill(1)
    half = toks // 2
    for step in range(1, full + 2):
        for d in (0, 1):
            origin = at(-2 * step) if d == 0 else at(2 * step)
            if step <= full:
                block = rows_of(origin)
            else:
                block = rows_of(origin, d * half, half)
            pltpu.make_async_remote_copy(
                src_ref=block, dst_ref=block, send_sem=asend.at[d, step - 1], recv_sem=arecv.at[d, step - 1],
                device_id={"tp": t}).wait_recv()
            if step < full:
                sent.append(remote(block, block, asend.at[d, step], arecv.at[d, step], tp=at(2 - 4 * d)))
            elif step == full:
                block = rows_of(origin, d * half, half)
                sent.append(remote(block, block, asend.at[d, step], arecv.at[d, step], tp=at(2 - 4 * d)))
            if step <= full:
                block = rows_of(origin)
                k = 2 * step - 1 + d
                sent.append(remote(block, block, apsend.at[k], aprecv.at[k], tp=mate))
        if step == 1:
            for d in (0, 1):
                sent.append(remote(kvbuf.at[y], kvbuf.at[y], ksend.at[d, 0], krecv.at[d, 0], tp=at(2 - 4 * d)))
        fill(1)
    last = 2 * full + 1
    block = rows_of(at(ring))
    sent.append(remote(block, block, apsend.at[last], aprecv.at[last], tp=mate))

    def landed(k):
        step, d = (k + 1) // 2, (k + 1) % 2
        origin = t if k == 0 else (at(-2 * step) if d == 0 else at(2 * step))
        if k == last:
            origin = at(ring)
        other = origin + 1 - 2 * core
        block = rows_of(other)
        pltpu.make_async_remote_copy(
            src_ref=block, dst_ref=block, send_sem=apsend.at[k], recv_sem=aprecv.at[k], device_id={"tp": t}).wait_recv()

    for k in range(last + 1):
        landed(k)

    tile = 256

    def product(j, rhs):
        @pl.loop(0, acts.shape[0] // tile)
        def _(m):
            r = pl.ds(mul(m, tile), tile)
            p = jnp.dot(acts[r, :], rhs(), preferred_element_type=F32)
            part[j, 0, r, :] = p[:, :HD]
            part[j, 1, r, :] = p[:, HD:]

    pairs = heads // 2
    todo = list(range(pairs))
    for step in range(1, full + 2):
        for d in (0, 1):
            steps = full + d
            if step > steps:
                continue
            origin = lax.rem(y - step + ring, ring) if d == 0 else lax.rem(y + step, ring)
            block = kvbuf.at[origin]
            pltpu.make_async_remote_copy(
                src_ref=block, dst_ref=block, send_sem=ksend.at[d, step - 1], recv_sem=krecv.at[d, step - 1],
                device_id={"tp": t}).wait_recv()
            if step < steps:
                sent.append(remote(block, block, ksend.at[d, step], krecv.at[d, step], tp=at(2 - 4 * d)))
        fill(2)
        if todo:
            j = todo.pop(0)
            product(j, lambda j=j: jnp.concatenate([qv[2 * j], qv[2 * j + 1]], axis=1))
    for j in todo:
        product(j, lambda j=j: jnp.concatenate([qv[2 * j], qv[2 * j + 1]], axis=1))
    fill(FILL)
    near = [k for k in range(len(dist)) if k not in (far, 0)] + [0]
    order = [(k, r) for r in range(cap) for k in near[:-1]] + [(0, r) for r in range(cap)]
    for k, r in order:
        i = k * cap + r
        sent.append(remote(sendq.at[i], qraw.at[i], qsend.at[i], qrecv.at[i], tp=at(dist[k])))

    kvraw[core] = kvbuf[kvt_ref[t]]
    kvsend[...] = kvbuf[kvt_ref[mate]]
    sent.append(remote(kvsend, kvraw.at[core], kpsend, kprecv, tp=mate))

    def rs_copy(j, d, s):
        b = lax.rem(x - 1 - s + 2 * subs, subs) if d == 0 else lax.rem(x + 1 + s, subs)
        block = part.shape[2] // subs
        return pltpu.make_async_remote_copy(
            src_ref=part.at[j, d, pl.ds(mul(b, block), block)], dst_ref=rsbuf.at[j, d, s],
            send_sem=rsend.at[j, d, s], recv_sem=rrecv.at[j, d, s],
            device_id={"sub": lax.rem(x + (1 if d == 0 else subs - 1), subs)})

    def rs_add(j, d, s):
        b = lax.rem(x - 2 - s + 2 * subs, subs) if d == 0 else lax.rem(x + 2 + s, subs)
        block = part.shape[2] // subs
        rs_copy(j, d, s).wait_recv()
        r = pl.ds(mul(b, block), block)
        part[j, d, r, :] += rsbuf[j, d, s]

    streams = [(j, d) for j in range(pairs + 1) for d in (0, 1)]
    for j, d in streams[:-2]:
        rs_copy(j, d, 0).start()
    pltpu.make_async_remote_copy(
        src_ref=kvsend, dst_ref=kvraw.at[1 - core], send_sem=kpsend, recv_sem=kprecv, device_id={"tp": t}).wait_recv()
    product(pairs, lambda: jnp.concatenate([kvraw[0], kvraw[1]], axis=1))
    for j, d in streams[-2:]:
        rs_copy(j, d, 0).start()

    @pl.loop(0, subs - 2)
    def _(s):
        ready = None
        for j, d in streams:
            rs_add(j, d, s)
            if ready is not None:
                rs_copy(*ready, s + 1).start()
            ready = (j, d)
        rs_copy(*ready, s + 1).start()

    mine = pl.ds(mul(x, part.shape[2] // subs), part.shape[2] // subs)
    for j, d in streams:
        rs_add(j, d, subs - 2)
        if j < pairs:
            res[2 * j + d] = part[j, d, mine, :].astype(BF16)
        else:
            kvres[d] = part[j, d, mine, :].astype(BF16)
    for i in range(heads):
        ssel[i] = res[sel_ref[i]]
    for i in range(heads):
        sent.append(remote(ssel.at[i], sraw.at[i], ss_send.at[i], ss_recv.at[i], tp=at(dist[i // cap])))

    @pl.loop(0, subs - 1)
    def _(s):
        for j, d in streams:
            rs_copy(j, d, s).wait_send()

    for copy in sent:
        copy.wait_send()
    for copy in fills:
        copy.wait()
    for k, r in order:
        i = k * cap + r
        pltpu.make_async_remote_copy(
            src_ref=sendq.at[i], dst_ref=qraw.at[i], send_sem=qsend.at[i], recv_sem=qrecv.at[i], device_id={"tp": t}).wait_recv()
    for i in range(heads):
        pltpu.make_async_remote_copy(
            src_ref=ssel.at[i], dst_ref=sraw.at[i], send_sem=ss_send.at[i], recv_sem=ss_recv.at[i], device_id={"tp": t}).wait_recv()


def place(gat, qraw, kvraw, sraw, kvres, q_new, kv_new, qkv, sem):
    heads = qraw.shape[0]
    copies = []
    for p in range(heads):
        cols = pl.ds(p * HD, HD)
        copies.append(pltpu.make_async_copy(qraw.at[gat[p]], q_new.at[:, cols], sem.at[0, p]))
        copies.append(pltpu.make_async_copy(sraw.at[gat[p]], qkv.at[:, cols], sem.at[1, p]))
    for p in range(2):
        copies.append(pltpu.make_async_copy(kvraw.at[p], kv_new.at[:, pl.ds(p * HD, HD)], sem.at[2, p]))
        copies.append(pltpu.make_async_copy(kvres.at[p], qkv.at[:, pl.ds((heads + p) * HD, HD)], sem.at[3, p]))
    for copy in copies:
        copy.start()
    for copy in copies:
        copy.wait()


def per_device(tp, subs, acts, q_src, kv_src, q_src_heads, q_tgt_heads, kv_tgt_heads):
    t = lax.axis_index("tp")
    toks, depth = acts.shape
    rows, heads = q_src.shape[0], q_src.shape[1] // HD
    dist, cap, stride = distances(tp, heads)
    own = jnp.arange(heads, dtype=jnp.int32)
    ids = jnp.arange(heads * tp, dtype=jnp.int32)

    def slot(block, other):
        held = lax.dynamic_slice_in_dim(block, t * heads, heads)
        return jnp.sum(jnp.where(held[:, None] == other[None, :], ids[None, :], 0), axis=1)

    def hop(d):
        return jnp.where(d % stride == 0, d // stride, 0)

    to = hop((slot(q_src_heads, q_tgt_heads) // heads - t) % tp)
    rank = jnp.sum((to[:, None] == to[None, :]) & (own[None, :] < own[:, None]), axis=1, dtype=jnp.int32)
    sel = jnp.sum(jnp.where((to * cap + rank)[None, :] == own[:, None], own[None, :], 0), axis=1, dtype=jnp.int32)
    pos = slot(q_tgt_heads, q_src_heads)
    come = hop((t - pos // heads) % tp)
    order = jnp.sum((come[:, None] == come[None, :]) & (pos[None, :] < pos[:, None]), axis=1, dtype=jnp.int32)
    gat = come * cap + order

    wide = rows, HD
    tokens = toks * tp
    block = tokens // subs
    ring = tp // 2
    full = ring // 2 - 1
    dma = pltpu.SemaphoreType.DMA
    vmem = pl.BlockSpec(memory_space=pltpu.VMEM)
    smem = pl.BlockSpec(memory_space=pltpu.SMEM)
    anyp = pl.BlockSpec(memory_space=pl.ANY)
    raw = pl.pallas_call(
        functools.partial(exchange, tp, subs),
        out_shape=(
            pltpu.VMEM((heads, *wide), BF16),
            pltpu.VMEM((2, *wide), BF16),
            pltpu.VMEM((heads, block, HD), BF16),
            pltpu.VMEM((2, block, HD), BF16),
        ),
        in_specs=[smem, smem, anyp, anyp, anyp],
        out_specs=(vmem, vmem, vmem, vmem),
        scratch_shapes=[
            pltpu.VMEM((tokens, depth), BF16),
            pltpu.VMEM((heads, *wide), BF16),
            pltpu.VMEM((heads, *wide), BF16),
            pltpu.VMEM((ring, *wide), BF16),
            pltpu.VMEM(wide, BF16),
            pltpu.VMEM((heads // 2 + 1, 2, tokens, HD), F32),
            pltpu.VMEM((heads // 2 + 1, 2, subs - 1, block, HD), F32),
            pltpu.VMEM((heads, block, HD), BF16),
            pltpu.VMEM((heads, block, HD), BF16),
            dma((2 + heads,)),
            dma((2, full + 1)),
            dma((2, full + 1)),
            dma((ring,)),
            dma((ring,)),
            dma((2, full + 1)),
            dma((2, full + 1)),
            dma,
            dma,
            dma((heads,)),
            dma((heads,)),
            dma((FILL,)),
            dma((FILL,)),
            dma((heads // 2 + 1, 2, subs - 1)),
            dma((heads // 2 + 1, 2, subs - 1)),
            dma((heads,)),
            dma((heads,)),
        ],
        compiler_params=pltpu.CompilerParams(
            collective_id=0, has_side_effects=True, vmem_limit_bytes=50 * 2**20),
        name="exchange",
    )(sel, kv_tgt_heads, acts, q_src, kv_src)
    return pl.pallas_call(
        place,
        out_shape=(
            jax.ShapeDtypeStruct(q_src.shape, BF16),
            jax.ShapeDtypeStruct((rows, 2 * HD), BF16),
            jax.ShapeDtypeStruct((block, (heads + 2) * HD), BF16),
        ),
        in_specs=[smem, anyp, anyp, anyp, anyp],
        out_specs=(anyp, anyp, anyp),
        scratch_shapes=[dma((4, heads))],
        compiler_params=pltpu.CompilerParams(vmem_limit_bytes=2**20),
        name="place",
    )(gat, *(pltpu.with_memory_space_constraint(a, pltpu.VMEM) for a in raw))


def solution(mesh):
    in_specs = (
        P(("rep", "tp"), "sub"),
        P(("rep", "sub"), "tp"),
        P(("rep", "sub"), "tp"),
        P(),
        P(),
        P(),
    )
    out_specs = (P(("rep", "sub"), "tp"), P(("rep", "sub"), "tp"), P(("rep", "sub"), "tp"))
    return jax.shard_map(
        functools.partial(per_device, mesh.shape["tp"], mesh.shape["sub"]),
        mesh=mesh, in_specs=in_specs, out_specs=out_specs, check_vma=False)
```

time: 310 us -> 206 us (0.66)
  waiting for transfers between devices: 203 us -> 0 us
  Pallas kernels: 0 us -> 201 us
  local copies, waits for them, and re-layouts: 48.4 us -> 1.46 us
  starting transfers between devices: 17.1 us -> 0 us
  between operations: 15.9 us -> 0.65 us
  other arithmetic: 14.7 us -> 2.71 us
  matrix products: 10.2 us -> 0 us
    pallas_call x0 -> x2, Pallas kernels: none -> 201 us  [the longest x1 198 us: per_device(): pl.pallas_call(functools.partial(exchange, tp, subs), out_shape=(pltpu.VM...]
    ppermute x4 -> x0, waiting for transfers between devices: 123 us -> none  [from_behind(): return lax.ppermute(block, axis, route)]
    reduce_scatter x1 -> x0, waiting for transfers between devices: 56.8 us -> none  [per_device(): lax.psum_scatter(jnp.dot(gathered, joined_cols, preferred_element_type=jn...]
    gather x7 -> x0, local copies, waits for them, and re-layouts: 24.1 us -> none  [the longest x4 11.8 us: per_device(): outgoing_piece = jnp.take(q_three, chosen_slots, axis=1)]
    all_gather x2 -> x0, waiting for transfers between devices: 21.9 us -> none  [the longest x1 21.9 us: per_device(): gathered = lax.all_gather(acts, 'tp', axis=0, tiled=True)]
    unnamed x7 -> x0, local copies, waits for them, and re-layouts: 17.1 us -> none
    ppermute x4 -> x0, starting transfers between devices: 16.9 us -> none  [from_behind(): return lax.ppermute(block, axis, route)]
    dot_general x1 -> x0, matrix products: 10.2 us -> none  [per_device(): jnp.dot(gathered, joined_cols, preferred_element_type=jnp.float32)]
  transfers between devices with their start and end apart: 7 -> 0, of which waited for: 4 -> 0; matrix products, arithmetic and copies ran while one was open for 19% -> 0% of each run, Pallas kernels for 0% -> 0%
where the time goes in v1:
time: 206 us
  Pallas kernels  201 us (98%)
  other arithmetic  2.71 us (1%)
    pallas_call x1, Pallas kernels, per_device(): pl.pallas_call(functools.partial(exchange, tp, subs), out_shape=(pltpu.VM...  198 us

profile of v1, /device:TPU:513, one launch (start us, length us, event | category | flops | bytes accessed | tf_op | source)
XLA Modules:
  0.0 205.9 jit_solution(7703822103127435642)
XLA Ops:
  0.6 0.7 dynamic_slice.7
  1.4 0.7 dynamic_slice.6
  2.1 0.8 select_reduce_fusion.2
  2.9 0.8 select_reduce_fusion.1
  3.8 0.2 convert_reduce_fusion.1
  4.0 0.2 convert_reduce_fusion
  4.2 0.6 select_reduce_fusion.sel_ref
  4.8 197.8 %exchange.1 = (bf16[8,2048,128]{2,1,0:T(8,128)(2,1)S(1)}, bf16[2,2048,128]{2,1,0:T(8,128)(2,1)S(1)}, bf16[8,128,128]{2,1,0:T(8,128)(2,1)S(1)}, bf16[2,128,128]{2,1,0:T(8,128)(2,1)S(1)}) custom-call(s32[8]{0:T(128)} %select_reduce_fusion.sel_ref, s32[16]{0:T(128)} %kvt_ref.1, bf16[64,2048]{1,0:T(8,128)(2,1)} %acts_ref.1, bf16[2048,1024]{1,0:T(8,128)(2,1)} %q_ref.1, ...), custom_call_target="tpu_custom_call" | custom-call | tf_op jit(solution)/shard_map/exchange/pallas_call | solution.py:281
  202.7 3.3 %place.1 = (bf16[2048,1024]{1,0:T(8,128)(2,1)}, bf16[2048,256]{1,0:T(8,128)(2,1)}, bf16[128,1280]{1,0:T(8,128)(2,1)}) custom-call(s32[8]{0:T(128)S(1)} %multiply_add_fusion.1.gat, bf16[8,2048,128]{2,1,0:T(8,128)(2,1)S(1)} %get-tuple-element.7.qraw, bf16[2,2048,128]{2,1,0:T(8,128)(2,1)S(1)} %get-tuple-element.8.kvraw, ...), custom_call_target="tpu_custom_call" | custom-call | tf_op jit(solution)/shard_map/place/pallas_call | solution.py:323
  (3 shorter events, 0.0 us)

commit v2 on v1

v2 whole, which is shorter than its diff:
```python
import functools

import jax
import jax.numpy as jnp
from jax import lax
from jax.experimental import pallas as pl
from jax.experimental.pallas import tpu as pltpu
from jax.sharding import PartitionSpec as P

HD = 128
F32, BF16 = jnp.float32, jnp.bfloat16
FILL = 16


def distances(tp, heads):
    capacity = max(2, heads // tp)
    select = heads // capacity
    stride = tp // select
    return [min(1, stride - 1)] + [k * stride for k in range(1, select)], capacity, stride


def routes(tp, t, heads, mine_ref, other_ref, out):
    _, cap, stride = distances(tp, heads)
    wanted = [mine_ref[t * heads + i] for i in range(heads)]

    def look(p, found):
        head = other_ref[p]
        return tuple(jnp.where(head == w, p, f) for w, f in zip(wanted, found))

    at = lax.fori_loop(0, heads * tp, look, (jnp.int32(0),) * heads, unroll=8)
    hops = []
    for pos in at:
        d = lax.rem(pos // heads - t + tp, tp)
        d = d if out else lax.rem(tp - d, tp)
        hops.append(jnp.where(lax.rem(d, stride) == 0, d // stride, 0))
    first = list(range(heads)) if out else at
    ranks = []
    for i in range(heads):
        before = [jnp.where((hops[j] == hops[i]) & (first[j] < first[i]), 1, 0) for j in range(heads) if j != i]
        ranks.append(hops[i] * cap + sum(before))
    return ranks


def mul(index, size):
    return pl.multiple_of(index * size, size)


def exchange(tp, subs, src_ref, tgt_ref, kvt_ref, acts_ref, q_ref, kv_ref, qraw, kvraw, sraw, kvres, gat,
             acts, qv, sendq, kvbuf, kvsend, part, rsbuf, res, ld, asend, arecv, apsend, aprecv,
             ksend, krecv, kpsend, kprecv, qsend, qrecv, fsend, frecv, rsend, rrecv, ss_send, ss_recv):
    t, x = lax.axis_index("tp"), lax.axis_index("sub")
    core, y = lax.rem(t, 2), t // 2
    ring = tp // 2
    full = ring // 2 - 1
    toks, rows = acts_ref.shape[0], q_ref.shape[0]
    heads = q_ref.shape[1] // HD
    dist, cap, _ = distances(tp, heads)
    mate = t + 1 - 2 * core

    def at(d):
        return lax.rem(t + d + tp, tp)

    def remote(src, dst, send, recv, **where):
        copy = pltpu.make_async_remote_copy(
            src_ref=src, dst_ref=dst, send_sem=send, recv_sem=recv, device_id=where)
        copy.start()
        return copy

    def rows_of(index, first=0, count=toks):
        return acts.at[pl.ds(mul(index, toks) + first, count)]

    loads = [
        pltpu.make_async_copy(acts_ref, rows_of(t), ld.at[0]),
        pltpu.make_async_copy(kv_ref, kvbuf.at[y], ld.at[1]),
    ] + [pltpu.make_async_copy(q_ref.at[:, pl.ds(i * HD, HD)], qv.at[i], ld.at[2 + i]) for i in range(heads)]
    for copy in loads:
        copy.start()
    barrier = pltpu.get_barrier_semaphore()
    peers = {1, tp - 1, 2, tp - 2} | set(dist) | {tp - d for d in dist}
    for d in sorted(peers):
        pl.semaphore_signal(barrier, inc=1, device_id={"tp": at(d)})
    for d in (1, subs - 1):
        pl.semaphore_signal(barrier, inc=1, device_id={"sub": lax.rem(x + d, subs)})
    for copy in loads[:2]:
        copy.wait()
    with jax.named_scope("barrier"):
        pl.semaphore_wait(barrier, len(peers) + 2)

    sent = []
    for d in (0, 1):
        sent.append(remote(rows_of(t), rows_of(t), asend.at[d, 0], arecv.at[d, 0], tp=at(2 - 4 * d)))
    sent.append(remote(rows_of(t), rows_of(t), apsend.at[0], aprecv.at[0], tp=mate))
    fills = []
    far = len(dist) // 2
    per_head = FILL // cap
    span = rows // per_head

    def fill(count):
        for _ in range(count):
            i = len(fills)
            if i == FILL:
                return
            head, piece = far * cap + i % cap, i // cap
            cut = pl.ds(piece * span, span)
            fills.append(remote(sendq.at[head, cut], qraw.at[head, cut], fsend.at[i], frecv.at[i], tp=at(dist[far])))

    place_of = routes(tp, t, heads, src_ref, tgt_ref, True)
    picks = [sum(jnp.where(r == i, slot, 0) for slot, r in enumerate(place_of)) for i in range(heads)]
    for copy in loads[2:]:
        copy.wait()
    with jax.named_scope("select"):
        for i in range(heads):
            sendq[i] = qv[picks[i]]
    fill(2)
    half = toks // 2
    for step in range(1, full + 2):
        for d in (0, 1):
            origin = at(-2 * step) if d == 0 else at(2 * step)
            if step <= full:
                block = rows_of(origin)
            else:
                block = rows_of(origin, d * half, half)
            with jax.named_scope(f"tokens{step}{d}"):
                pltpu.make_async_remote_copy(
                    src_ref=block, dst_ref=block, send_sem=asend.at[d, step - 1], recv_sem=arecv.at[d, step - 1],
                    device_id={"tp": t}).wait_recv()
            if step < full:
                sent.append(remote(block, block, asend.at[d, step], arecv.at[d, step], tp=at(2 - 4 * d)))
            elif step == full:
                block = rows_of(origin, d * half, half)
                sent.append(remote(block, block, asend.at[d, step], arecv.at[d, step], tp=at(2 - 4 * d)))
            if step <= full:
                block = rows_of(origin)
                k = 2 * step - 1 + d
                sent.append(remote(block, block, apsend.at[k], aprecv.at[k], tp=mate))
        if step == 1:
            for d in (0, 1):
                sent.append(remote(kvbuf.at[y], kvbuf.at[y], ksend.at[d, 0], krecv.at[d, 0], tp=at(2 - 4 * d)))
        fill(2)
    last = 2 * full + 1
    block = rows_of(at(ring))
    sent.append(remote(block, block, apsend.at[last], aprecv.at[last], tp=mate))

    def landed(k):
        step, d = (k + 1) // 2, (k + 1) % 2
        origin = t if k == 0 else (at(-2 * step) if d == 0 else at(2 * step))
        if k == last:
            origin = at(ring)
        other = origin + 1 - 2 * core
        block = rows_of(other)
        pltpu.make_async_remote_copy(
            src_ref=block, dst_ref=block, send_sem=apsend.at[k], recv_sem=aprecv.at[k], device_id={"tp": t}).wait_recv()

    with jax.named_scope("mate"):
        for k in range(last + 1):
            landed(k)

    tile = 256

    def product(j, rhs):
        @pl.loop(0, acts.shape[0] // tile)
        def _(m):
            r = pl.ds(mul(m, tile), tile)
            p = jnp.dot(acts[r, :], rhs(), preferred_element_type=F32)
            part[j, 0, r, :] = p[:, :HD]
            part[j, 1, r, :] = p[:, HD:]

    pairs = heads // 2
    todo = [j for j in range(pairs) if j != far]

    def rs_copy(j, d, s):
        b = lax.rem(x - 1 - s + 2 * subs, subs) if d == 0 else lax.rem(x + 1 + s, subs)
        block = part.shape[2] // subs
        return pltpu.make_async_remote_copy(
            src_ref=part.at[j, d, pl.ds(mul(b, block), block)], dst_ref=rsbuf.at[j, d, s],
            send_sem=rsend.at[j, d, s], recv_sem=rrecv.at[j, d, s],
            device_id={"sub": lax.rem(x + (1 if d == 0 else subs - 1), subs)})

    def rs_add(j, d, s):
        b = lax.rem(x - 2 - s + 2 * subs, subs) if d == 0 else lax.rem(x + 2 + s, subs)
        block = part.shape[2] // subs
        rs_copy(j, d, s).wait_recv()
        r = pl.ds(mul(b, block), block)
        part[j, d, r, :] += rsbuf[j, d, s]

    def pair(ref, j):
        return jnp.concatenate([ref[2 * j], ref[2 * j + 1]], axis=1)

    def here(j):
        with jax.named_scope(f"product{j}"):
            product(j, lambda: pair(sendq, j))
        for d in (0, 1):
            rs_copy(j, d, 0).start()

    def rs_step(streams, s):
        with jax.named_scope(f"reduce{s}"):
            ready = None
            for j, d in streams:
                rs_add(j, d, s)
                if s == subs - 2:
                    total = part[j, d, mine, :].astype(BF16)
                    if j == pairs:
                        kvres[d] = total
                    elif j == far:
                        sraw[2 * j + d] = total
                    else:
                        res[2 * j + d] = total
                    continue
                if ready is not None:
                    rs_copy(*ready, s + 1).start()
                ready = (j, d)
            if ready is not None:
                rs_copy(*ready, s + 1).start()

    mine = pl.ds(mul(x, part.shape[2] // subs), part.shape[2] // subs)
    early = [(j, d) for j in todo for d in (0, 1)]
    late = [(j, d) for j in (pairs, far) for d in (0, 1)]

    def straight(k):
        for r in range(cap):
            i = k * cap + r
            sent.append(remote(sendq.at[i], qraw.at[i], qsend.at[i], qrecv.at[i], tp=at(dist[k])))

    near = [k for k in range(1, len(dist)) if k != far]
    done = 0
    for step in range(1, full + 2):
        for d in (0, 1):
            steps = full + d
            if step > steps:
                continue
            origin = lax.rem(y - step + ring, ring) if d == 0 else lax.rem(y + step, ring)
            block = kvbuf.at[origin]
            with jax.named_scope(f"kv{step}{d}"):
                pltpu.make_async_remote_copy(
                    src_ref=block, dst_ref=block, send_sem=ksend.at[d, step - 1], recv_sem=krecv.at[d, step - 1],
                    device_id={"tp": t}).wait_recv()
            if step < steps:
                sent.append(remote(block, block, ksend.at[d, step], krecv.at[d, step], tp=at(2 - 4 * d)))
        fill(2)
        if step == full:
            straight(0)
        if step == 1:
            for j in todo:
                here(j)
        elif step <= full:
            for _ in range(2):
                rs_step(early, done)
                done += 1
    fill(FILL)
    for k in near:
        straight(k)
    kvraw[core] = kvbuf[kvt_ref[t]]
    kvsend[...] = kvbuf[kvt_ref[mate]]
    sent.append(remote(kvsend, kvraw.at[core], kpsend, kprecv, tp=mate))
    rs_step(early, done)
    pltpu.make_async_remote_copy(
        src_ref=kvsend, dst_ref=kvraw.at[1 - core], send_sem=kpsend, recv_sem=kprecv, device_id={"tp": t}).wait_recv()
    product(pairs, lambda: pair(kvraw, 0))
    for d in (0, 1):
        rs_copy(pairs, d, 0).start()
    for s in range(done + 1, subs - 1):
        rs_step(early, s)
    back = [i for i in range(heads) if i // cap != far]
    for i in back:
        sent.append(remote(res.at[i], sraw.at[i], ss_send.at[i], ss_recv.at[i], tp=at(dist[i // cap])))
    for i, r in enumerate(routes(tp, t, heads, tgt_ref, src_ref, False)):
        gat[i] = r
    with jax.named_scope("far"):
        for copy in fills:
            copy.wait_recv()
    product(far, lambda: pair(qraw, far))
    for d in (0, 1):
        rs_copy(far, d, 0).start()
    for s in range(subs - 1):
        rs_step(late, s)

    @pl.loop(0, subs - 1)
    def _(s):
        for j, d in early + late:
            rs_copy(j, d, s).wait_send()

    with jax.named_scope("sent"):
        for copy in sent:
            copy.wait_send()
    for copy in fills:
        copy.wait_send()
    for i in back:
        with jax.named_scope(f"head{i}"):
            pltpu.make_async_remote_copy(
                src_ref=sendq.at[i], dst_ref=qraw.at[i], send_sem=qsend.at[i], recv_sem=qrecv.at[i], device_id={"tp": t}).wait_recv()
    with jax.named_scope("back"):
        for i in back:
            pltpu.make_async_remote_copy(
                src_ref=res.at[i], dst_ref=sraw.at[i], send_sem=ss_send.at[i], recv_sem=ss_recv.at[i], device_id={"tp": t}).wait_recv()


def place(gat, qraw, kvraw, sraw, kvres, q_new, kv_new, qkv, sem):
    heads = qraw.shape[0]
    copies = []
    for p in range(heads):
        cols = pl.ds(p * HD, HD)
        copies.append(pltpu.make_async_copy(qraw.at[gat[p]], q_new.at[:, cols], sem.at[0, p]))
        copies.append(pltpu.make_async_copy(sraw.at[gat[p]], qkv.at[:, cols], sem.at[1, p]))
    for p in range(2):
        copies.append(pltpu.make_async_copy(kvraw.at[p], kv_new.at[:, pl.ds(p * HD, HD)], sem.at[2, p]))
        copies.append(pltpu.make_async_copy(kvres.at[p], qkv.at[:, pl.ds((heads + p) * HD, HD)], sem.at[3, p]))
    for copy in copies:
        copy.start()
    for copy in copies:
        copy.wait()


def per_device(tp, subs, acts, q_src, kv_src, q_src_heads, q_tgt_heads, kv_tgt_heads):
    toks, depth = acts.shape
    rows, heads = q_src.shape[0], q_src.shape[1] // HD
    wide = rows, HD
    tokens = toks * tp
    block = tokens // subs
    ring = tp // 2
    full = ring // 2 - 1
    dma = pltpu.SemaphoreType.DMA
    vmem = pl.BlockSpec(memory_space=pltpu.VMEM)
    smem = pl.BlockSpec(memory_space=pltpu.SMEM)
    anyp = pl.BlockSpec(memory_space=pl.ANY)
    *raw, gat = pl.pallas_call(
        functools.partial(exchange, tp, subs),
        out_shape=(
            pltpu.VMEM((heads, *wide), BF16),
            pltpu.VMEM((2, *wide), BF16),
            pltpu.VMEM((heads, block, HD), BF16),
            pltpu.VMEM((2, block, HD), BF16),
            jax.ShapeDtypeStruct((heads,), jnp.int32),
        ),
        in_specs=[smem, smem, smem, anyp, anyp, anyp],
        out_specs=(vmem, vmem, vmem, vmem, smem),
        scratch_shapes=[
            pltpu.VMEM((tokens, depth), BF16),
            pltpu.VMEM((heads, *wide), BF16),
            pltpu.VMEM((heads, *wide), BF16),
            pltpu.VMEM((ring, *wide), BF16),
            pltpu.VMEM(wide, BF16),
            pltpu.VMEM((heads // 2 + 1, 2, tokens, HD), F32),
            pltpu.VMEM((heads // 2 + 1, 2, subs - 1, block, HD), F32),
            pltpu.VMEM((heads, block, HD), BF16),
            dma((2 + heads,)),
            dma((2, full + 1)),
            dma((2, full + 1)),
            dma((ring,)),
            dma((ring,)),
            dma((2, full + 1)),
            dma((2, full + 1)),
            dma,
            dma,
            dma((heads,)),
            dma((heads,)),
            dma((FILL,)),
            dma((FILL,)),
            dma((heads // 2 + 1, 2, subs - 1)),
            dma((heads // 2 + 1, 2, subs - 1)),
            dma((heads,)),
            dma((heads,)),
        ],
        compiler_params=pltpu.CompilerParams(
            collective_id=0, has_side_effects=True, vmem_limit_bytes=50 * 2**20),
        name="exchange",
    )(q_src_heads, q_tgt_heads, kv_tgt_heads, acts, q_src, kv_src)
    return pl.pallas_call(
        place,
        out_shape=(
            jax.ShapeDtypeStruct(q_src.shape, BF16),
            jax.ShapeDtypeStruct((rows, 2 * HD), BF16),
            jax.ShapeDtypeStruct((block, (heads + 2) * HD), BF16),
        ),
        in_specs=[smem, anyp, anyp, anyp, anyp],
        out_specs=(anyp, anyp, anyp),
        scratch_shapes=[dma((4, heads))],
        compiler_params=pltpu.CompilerParams(vmem_limit_bytes=2**20),
        name="place",
    )(gat, *(pltpu.with_memory_space_constraint(a, pltpu.VMEM) for a in raw))


def solution(mesh):
    in_specs = (
        P(("rep", "tp"), "sub"),
        P(("rep", "sub"), "tp"),
        P(("rep", "sub"), "tp"),
        P(),
        P(),
        P(),
    )
    out_specs = (P(("rep", "sub"), "tp"), P(("rep", "sub"), "tp"), P(("rep", "sub"), "tp"))
    return jax.shard_map(
        functools.partial(per_device, mesh.shape["tp"], mesh.shape["sub"]),
        mesh=mesh, in_specs=in_specs, out_specs=out_specs, check_vma=False)
```

time: 206 us -> 196 us (0.951)
  Pallas kernels: 201 us -> 195 us
  other arithmetic: 2.71 us -> 0 us
    pallas_call x1, Pallas kernels: 198 us -> 192 us  [per_device(): pl.pallas_call(functools.partial(exchange, tp, subs), out_shape=(pltpu.VM...]
    reduce_sum x5 -> x0, other arithmetic: 2.67 us -> none  [the longest x2 1.67 us: slot(): jnp.sum(jnp.where(held[:, None] == other[None, :], ids[None, :], 0), axis=1)]
where the time goes in v2:
time: 196 us
  Pallas kernels  195 us (99%)
    pallas_call x1, Pallas kernels, per_device(): pl.pallas_call(functools.partial(exchange, tp, subs), out_shape=(pltpu.VM...  192 us

profile of v2, /device:TPU:513, one launch (start us, length us, event | category | flops | bytes accessed | tf_op | source)
XLA Modules:
  0.0 196.1 jit_solution(16823379159394933683)
XLA Ops:
  0.6 191.6 %exchange.1 = (bf16[8,2048,128]{2,1,0:T(8,128)(2,1)S(1)}, bf16[2,2048,128]{2,1,0:T(8,128)(2,1)S(1)}, bf16[8,128,128]{2,1,0:T(8,128)(2,1)S(1)}, bf16[2,128,128]{2,1,0:T(8,128)(2,1)S(1)}, s32[8]{0:T(128)}) custom-call(s32[128]{0:T(128)} %src_ref.1, s32[128]{0:T(128)} %tgt_ref.1, s32[16]{0:T(128)} %kvt_ref.1, bf16[64,2048]{1,0:T(8,128)(2,1)} %acts_ref.1, ...), custom_call_target="tpu_custom_call" | custom-call | tf_op jit(solution)/shard_map/exchange/pallas_call | solution.py:325
  192.2 0.0 copy-start
  192.2 0.6 copy-done
  192.8 3.2 %place.1 = (bf16[2048,1024]{1,0:T(8,128)(2,1)}, bf16[2048,256]{1,0:T(8,128)(2,1)}, bf16[128,1280]{1,0:T(8,128)(2,1)}) custom-call(s32[8]{0:T(128)S(1)} %copy-done, bf16[8,2048,128]{2,1,0:T(8,128)(2,1)S(1)} %get-tuple-element.9.qraw, bf16[2,2048,128]{2,1,0:T(8,128)(2,1)S(1)} %get-tuple-element.10.kvraw, bf16[8,128,128]{2,1,0:T(8,128)(2,1)S(1)} %get-tuple-element.11.sraw, ...), custom_call_target="tpu_custom_call" | custom-call | tf_op jit(solution)/shard_map/place/pallas_call | solution.py:367
Async XLA Ops:
  192.2 0.6 copy-start

commit v3 on v2

v3 whole, which is shorter than its diff:
```python
import functools

import jax
import jax.numpy as jnp
from jax import lax
from jax.experimental import pallas as pl
from jax.experimental.pallas import tpu as pltpu
from jax.sharding import PartitionSpec as P

HD = 128
F32, BF16 = jnp.float32, jnp.bfloat16
FILL = 16
FILL0, FILL1 = 2, 4
Q1 = 3
LEG = 2


def distances(tp, heads):
    capacity = max(2, heads // tp)
    select = heads // capacity
    stride = tp // select
    return [min(1, stride - 1)] + [k * stride for k in range(1, select)], capacity, stride


def routes(tp, t, heads, mine_ref, other_ref, out):
    _, cap, stride = distances(tp, heads)
    wanted = [mine_ref[t * heads + i] for i in range(heads)]

    def look(p, found):
        head = other_ref[p]
        return tuple(jnp.where(head == w, p, f) for w, f in zip(wanted, found))

    at = lax.fori_loop(0, heads * tp, look, (jnp.int32(0),) * heads, unroll=8)
    hops = []
    for pos in at:
        d = lax.rem(pos // heads - t + tp, tp)
        d = d if out else lax.rem(tp - d, tp)
        hops.append(jnp.where(lax.rem(d, stride) == 0, d // stride, 0))
    first = list(range(heads)) if out else at
    ranks = []
    for i in range(heads):
        before = [jnp.where((hops[j] == hops[i]) & (first[j] < first[i]), 1, 0) for j in range(heads) if j != i]
        ranks.append(hops[i] * cap + sum(before))
    return ranks


def mul(index, size):
    return pl.multiple_of(index * size, size)


def exchange(tp, subs, src_ref, tgt_ref, kvt_ref, acts_ref, q_ref, kv_ref, qraw, kvraw, sraw, kvres, gat_ref,
             gat, acts, qv, sendq, kvown, kvbuf, kvsend, part, rsbuf, res, ld, asend, arecv, apsend, aprecv,
             k1send, k1recv, k2send, k2recv, qsend, qrecv, rsend, rrecv, ss_send, ss_recv):
    t, x = lax.axis_index("tp"), lax.axis_index("sub")
    core, y = lax.rem(t, 2), t // 2
    ring = tp // 2
    full = ring // 2 - 1
    toks, rows = acts_ref.shape[0], q_ref.shape[0]
    heads = q_ref.shape[1] // HD
    pairs = heads // 2
    dist, cap, _ = distances(tp, heads)
    far = len(dist) // 2
    near = [k for k in range(1, len(dist)) if k != far]
    mate = t + 1 - 2 * core
    piece = rows // ring
    block = acts.shape[0] // subs

    def at(d):
        return lax.rem(t + d + 2 * tp, tp)

    def chip(d):
        return lax.rem(y + d + ring, ring)

    def describe(src, dst, send, recv, **where):
        return pltpu.make_async_remote_copy(
            src_ref=src, dst_ref=dst, send_sem=send, recv_sem=recv, device_id=where)

    def remote(src, dst, send, recv, **where):
        describe(src, dst, send, recv, **where).start()

    def arrived(dst, send, recv):
        describe(dst, dst, send, recv, tp=t).wait_recv()

    def tokens_of(index):
        return acts.at[pl.ds(mul(index, toks), toks)]

    def rows_of(index):
        return pl.ds(mul(index, piece), piece)

    loads = [
        pltpu.make_async_copy(acts_ref, tokens_of(t), ld.at[0]),
        pltpu.make_async_copy(kv_ref, kvown, ld.at[1]),
        pltpu.make_async_copy(kv_ref.at[rows_of(y)], kvbuf.at[y], ld.at[2]),
    ] + [pltpu.make_async_copy(q_ref.at[:, pl.ds(i * HD, HD)], qv.at[i], ld.at[3]) for i in range(heads)]
    for copy in loads:
        copy.start()
    barrier = pltpu.get_barrier_semaphore()
    for d in range(1, tp):
        pl.semaphore_signal(barrier, inc=1, device_id={"tp": at(d)})
    for d in (1, subs - 1):
        pl.semaphore_signal(barrier, inc=1, device_id={"sub": lax.rem(x + d, subs)})
    for copy in loads[:3]:
        copy.wait()
    with jax.named_scope("barrier"):
        pl.semaphore_wait(barrier, tp + 1)

    def tokens(d, step, origin):
        remote(tokens_of(origin), tokens_of(origin), asend, arecv.at[d, step], tp=at(2 - 4 * d))

    def hand(origin):
        remote(tokens_of(origin), tokens_of(origin), apsend, aprecv, tp=mate)

    tokens(0, 0, t)
    tokens(1, 0, t)
    hand(t)
    for d in range(1, ring):
        remote(kvown.at[rows_of(chip(d))], kvbuf.at[y], k1send, k1recv, tp=at(2 * d))

    place_of = routes(tp, t, heads, src_ref, tgt_ref, True)
    picks = [sum(jnp.where(r == i, slot, 0) for slot, r in enumerate(place_of)) for i in range(heads)]
    pltpu.make_async_copy(qv, qv, ld.at[3]).wait()
    with jax.named_scope("select"):
        for i in range(heads):
            sendq[i] = qv[picks[i]]

    fills = []
    per_head = FILL // cap
    span = rows // per_head

    def fill(count):
        start = len(fills)
        for n in range(start, min(start + count, FILL)):
            fills.append(n)
            for f, k in enumerate(near):
                head, cut = k * cap + n // per_head, pl.ds(n % per_head * span, span)
                remote(sendq.at[head, cut], qraw.at[head, cut], qsend, qrecv, tp=at(dist[k]))

    def straight(k):
        for i in range(k * cap, (k + 1) * cap):
            remote(sendq.at[i], qraw.at[i], qsend, qrecv, tp=at(dist[k]))

    def second_leg():
        with jax.named_scope("leg1"):
            arrived(kvbuf.at[pl.ds(1, ring - 1)], k1send, k1recv)
        for d in range(1, tp):
            kvsend[d] = kvbuf[kvt_ref[at(d)]]
        kvraw[core, rows_of(y), :] = kvbuf[kvt_ref[t]]
        for d in sorted(range(1, tp), key=lambda d: -min(d, tp - d)):
            remote(kvsend.at[d], kvraw.at[core, rows_of(y)], k2send, k2recv, tp=at(d))

    fill(FILL0)
    for step in range(1, full + 2):
        for d in (0, 1):
            if step > full + d:
                continue
            origin = at(-2 * step) if d == 0 else at(2 * step)
            with jax.named_scope(f"tokens{step}{d}"):
                arrived(tokens_of(origin), asend, arecv.at[d, step - 1])
            if step < full + d:
                tokens(d, step, origin)
            hand(origin)
        if step == LEG:
            second_leg()
        fill(FILL1)
        if step == Q1:
            straight(0)

    tile = 256

    def product(j, ref, first):
        with jax.named_scope(f"product{j}"):
            @pl.loop(0, acts.shape[0] // tile)
            def _(m):
                r = pl.ds(mul(m, tile), tile)
                rhs = jnp.concatenate([ref[first], ref[first + 1]], axis=1)
                p = jnp.dot(acts[r, :], rhs, preferred_element_type=F32)
                part[j, 0, r, :] = p[:, :HD]
                part[j, 1, r, :] = p[:, HD:]
        for d in (0, 1):
            rs_copy(j, d, 0).start()

    def part_of(b):
        return pl.ds(mul(b, block), block)

    def rs_copy(j, d, s):
        b = lax.rem(x - 1 - s + 2 * subs, subs) if d == 0 else lax.rem(x + 1 + s, subs)
        return describe(part.at[j, d, part_of(b)], rsbuf.at[j, d, s], rsend.at[j, d], rrecv.at[j, d, s],
                        sub=lax.rem(x + (1 if d == 0 else subs - 1), subs))

    def rs_step(group, s):
        with jax.named_scope(f"reduce{s}"):
            ready = None
            for j in group:
                for d in (0, 1):
                    b = lax.rem(x - 2 - s + 2 * subs, subs) if d == 0 else lax.rem(x + 2 + s, subs)
                    rs_copy(j, d, s).wait_recv()
                    total = part[j, d, part_of(b), :] + rsbuf[j, d, s]
                    if s == subs - 2:
                        total = total.astype(BF16)
                        if j == pairs:
                            kvres[d] = total
                        else:
                            res[2 * j + d] = total
                        continue
                    part[j, d, part_of(b), :] = total
                    rs_copy(j, d, s).wait_send()
                    if ready is not None:
                        rs_copy(*ready, s + 1).start()
                    ready = (j, d)
            if ready is not None:
                rs_copy(*ready, s + 1).start()

    with jax.named_scope("mate"):
        arrived(acts.at[pl.ds(0, ring * toks)], apsend, aprecv)

    for k in range(pairs):
        product(k, sendq, k * cap)
    with jax.named_scope("leg2"):
        arrived(kvsend.at[pl.ds(1, tp - 1)], k2send, k2recv)
    product(pairs, kvraw, 0)
    fill(FILL)
    straight(far)
    group = list(range(pairs + 1))
    for s in range(subs - 1):
        rs_step(group, s)
    back = range(heads)
    for i in back:
        remote(res.at[i], sraw.at[i], ss_send, ss_recv, tp=at(dist[i // cap]))
    for i, r in enumerate(routes(tp, t, heads, tgt_ref, src_ref, False)):
        gat[i] = r
    table = pltpu.make_async_copy(gat, gat_ref, ld.at[0])
    table.start()
    for j in group:
        for d in (0, 1):
            rs_copy(j, d, subs - 2).wait_send()

    table.wait()
    with jax.named_scope("sent"):
        for src, sem in ((acts.at[pl.ds(0, (2 * full + 1) * toks)], asend), (acts.at[pl.ds(0, ring * toks)], apsend),
                         (kvbuf.at[pl.ds(1, ring - 1)], k1send), (kvsend.at[pl.ds(1, tp - 1)], k2send),
                         (sendq, qsend), (res, ss_send)):
            describe(src, src, sem, sem, tp=t).wait_send()
    with jax.named_scope("heads"):
        arrived(qraw, qsend, qrecv)
    with jax.named_scope("back"):
        arrived(sraw, ss_send, ss_recv)


def place(gat, qraw, kvraw, sraw, kvres, q_new, kv_new, qkv, sem):
    heads = qraw.shape[0]
    copies = []
    for p in range(heads):
        cols = pl.ds(p * HD, HD)
        copies.append(pltpu.make_async_copy(qraw.at[gat[p]], q_new.at[:, cols], sem.at[0, p]))
        copies.append(pltpu.make_async_copy(sraw.at[gat[p]], qkv.at[:, cols], sem.at[1, p]))
    for p in range(2):
        copies.append(pltpu.make_async_copy(kvraw.at[p], kv_new.at[:, pl.ds(p * HD, HD)], sem.at[2, p]))
        copies.append(pltpu.make_async_copy(kvres.at[p], qkv.at[:, pl.ds((heads + p) * HD, HD)], sem.at[3, p]))
    for copy in copies:
        copy.start()
    for copy in copies:
        copy.wait()


def per_device(tp, subs, acts, q_src, kv_src, q_src_heads, q_tgt_heads, kv_tgt_heads):
    toks, depth = acts.shape
    rows, heads = q_src.shape[0], q_src.shape[1] // HD
    dist, _, _ = distances(tp, heads)
    wide = rows, HD
    tokens = toks * tp
    block = tokens // subs
    ring = tp // 2
    full = ring // 2 - 1
    dma = pltpu.SemaphoreType.DMA
    vmem = pl.BlockSpec(memory_space=pltpu.VMEM)
    smem = pl.BlockSpec(memory_space=pltpu.SMEM)
    anyp = pl.BlockSpec(memory_space=pl.ANY)
    *raw, gat = pl.pallas_call(
        functools.partial(exchange, tp, subs),
        out_shape=(
            pltpu.VMEM((heads, *wide), BF16),
            pltpu.VMEM((2, *wide), BF16),
            pltpu.VMEM((heads, block, HD), BF16),
            pltpu.VMEM((2, block, HD), BF16),
            jax.ShapeDtypeStruct((heads,), jnp.int32),
        ),
        in_specs=[smem, smem, smem, anyp, anyp, anyp],
        out_specs=(vmem, vmem, vmem, vmem, anyp),
        scratch_shapes=[
            pltpu.SMEM((heads,), jnp.int32),
            pltpu.VMEM((tokens, depth), BF16),
            pltpu.VMEM((heads, *wide), BF16),
            pltpu.VMEM((heads, *wide), BF16),
            pltpu.VMEM(wide, BF16),
            pltpu.VMEM((ring, rows // ring, HD), BF16),
            pltpu.VMEM((tp, rows // ring, HD), BF16),
            pltpu.VMEM((heads // 2 + 1, 2, tokens, HD), F32),
            pltpu.VMEM((heads // 2 + 1, 2, subs - 1, block, HD), F32),
            pltpu.VMEM((heads, block, HD), BF16),
            dma((4,)),
            dma,
            dma((2, full + 1)),
            *[dma] * 8,
            dma((heads // 2 + 1, 2)),
            dma((heads // 2 + 1, 2, subs - 1)),
            dma,
            dma,
        ],
        compiler_params=pltpu.CompilerParams(
            collective_id=0, has_side_effects=True, vmem_limit_bytes=50 * 2**20),
        name="exchange",
    )(q_src_heads, q_tgt_heads, kv_tgt_heads, acts, q_src, kv_src)
    return pl.pallas_call(
        place,
        out_shape=(
            jax.ShapeDtypeStruct(q_src.shape, BF16),
            jax.ShapeDtypeStruct((rows, 2 * HD), BF16),
            jax.ShapeDtypeStruct((block, (heads + 2) * HD), BF16),
        ),
        in_specs=[smem, anyp, anyp, anyp, anyp],
        out_specs=(anyp, anyp, anyp),
        scratch_shapes=[dma((4, heads))],
        compiler_params=pltpu.CompilerParams(vmem_limit_bytes=2**20),
        name="place",
    )(gat, *(pltpu.with_memory_space_constraint(a, pltpu.VMEM) for a in raw))


def solution(mesh):
    in_specs = (
        P(("rep", "tp"), "sub"),
        P(("rep", "sub"), "tp"),
        P(("rep", "sub"), "tp"),
        P(),
        P(),
        P(),
    )
    out_specs = (P(("rep", "sub"), "tp"), P(("rep", "sub"), "tp"), P(("rep", "sub"), "tp"))
    return jax.shard_map(
        functools.partial(per_device, mesh.shape["tp"], mesh.shape["sub"]),
        mesh=mesh, in_specs=in_specs, out_specs=out_specs, check_vma=False)
```

time: 196 us -> 191 us (0.974)
  Pallas kernels: 195 us -> 189 us
    pallas_call x1, Pallas kernels: 192 us -> 186 us  [per_device(): pl.pallas_call(functools.partial(exchange, tp, subs), out_shape=(pltpu.VM...]
where the time goes in v3:
time: 191 us; the launch traced here: 190 us
  Pallas kernels  189 us (99%)
    pallas_call x1, Pallas kernels, per_device(): pl.pallas_call(functools.partial(exchange, tp, subs), out_shape=(pltpu.VM...  186 us

profile of v3, /device:TPU:513, one launch (start us, length us, event | category | flops | bytes accessed | tf_op | source)
XLA Modules:
  0.0 190.4 jit_solution(230749211634662262)
XLA Ops:
  0.6 185.9 %exchange.1 = (bf16[8,2048,128]{2,1,0:T(8,128)(2,1)S(1)}, bf16[2,2048,128]{2,1,0:T(8,128)(2,1)S(1)}, bf16[8,128,128]{2,1,0:T(8,128)(2,1)S(1)}, bf16[2,128,128]{2,1,0:T(8,128)(2,1)S(1)}, s32[8]{0:T(128)}) custom-call(s32[128]{0:T(128)} %src_ref.1, s32[128]{0:T(128)} %tgt_ref.1, s32[16]{0:T(128)} %kvt_ref.1, bf16[64,2048]{1,0:T(8,128)(2,1)} %acts_ref.1, ...), custom_call_target="tpu_custom_call" | custom-call | tf_op jit(solution)/shard_map/exchange/pallas_call | solution.py:278
  186.5 0.0 copy-start
  186.5 0.6 copy-done
  187.1 3.2 %place.1 = (bf16[2048,1024]{1,0:T(8,128)(2,1)}, bf16[2048,256]{1,0:T(8,128)(2,1)}, bf16[128,1280]{1,0:T(8,128)(2,1)}) custom-call(s32[8]{0:T(128)S(1)} %copy-done, bf16[8,2048,128]{2,1,0:T(8,128)(2,1)S(1)} %get-tuple-element.9.qraw, bf16[2,2048,128]{2,1,0:T(8,128)(2,1)S(1)} %get-tuple-element.10.kvraw, bf16[8,128,128]{2,1,0:T(8,128)(2,1)S(1)} %get-tuple-element.11.sraw, ...), custom_call_target="tpu_custom_call" | custom-call | tf_op jit(solution)/shard_map/place/pallas_call | solution.py:313
Async XLA Ops:
  186.5 0.6 copy-start

commit v4 on v3

--- a/solution.py
+++ b/solution.py
@@ -10,9 +10,9 @@
 HD = 128
 F32, BF16 = jnp.float32, jnp.bfloat16
 FILL = 16
-FILL0, FILL1 = 2, 4
-Q1 = 3
-LEG = 2
+FILL1, FILL2 = 2, 3
+Q1 = 2
+AHEAD = 2
 
 
 def distances(tp, heads):
@@ -95,26 +95,32 @@
     for copy in loads:
         copy.start()
     barrier = pltpu.get_barrier_semaphore()
-    for d in range(1, tp):
-        pl.semaphore_signal(barrier, inc=1, device_id={"tp": at(d)})
+    for peer in (at(2), at(-2), mate):
+        pl.semaphore_signal(barrier, inc=1, device_id={"tp": peer})
     for d in (1, subs - 1):
         pl.semaphore_signal(barrier, inc=1, device_id={"sub": lax.rem(x + d, subs)})
     for copy in loads[:3]:
         copy.wait()
     with jax.named_scope("barrier"):
-        pl.semaphore_wait(barrier, tp + 1)
+        pl.semaphore_wait(barrier, 5)
 
     def tokens(d, step, origin):
         remote(tokens_of(origin), tokens_of(origin), asend, arecv.at[d, step], tp=at(2 - 4 * d))
 
-    def hand(origin):
-        remote(tokens_of(origin), tokens_of(origin), apsend, aprecv, tp=mate)
+    def hand(k, origin):
+        remote(tokens_of(origin), tokens_of(origin), apsend, aprecv.at[k], tp=mate)
+
+    def handed(k, origin):
+        arrived(tokens_of(origin + 1 - 2 * core), apsend, aprecv.at[k])
 
     tokens(0, 0, t)
     tokens(1, 0, t)
-    hand(t)
-    for d in range(1, ring):
+    hand(0, t)
+    def first_leg(d):
         remote(kvown.at[rows_of(chip(d))], kvbuf.at[y], k1send, k1recv, tp=at(2 * d))
+
+    first_leg(1)
+    first_leg(-1)
 
     place_of = routes(tp, t, heads, src_ref, tgt_ref, True)
     picks = [sum(jnp.where(r == i, slot, 0) for slot, r in enumerate(place_of)) for i in range(heads)]
@@ -148,7 +154,6 @@
         for d in sorted(range(1, tp), key=lambda d: -min(d, tp - d)):
             remote(kvsend.at[d], kvraw.at[core, rows_of(y)], k2send, k2recv, tp=at(d))
 
-    fill(FILL0)
     for step in range(1, full + 2):
         for d in (0, 1):
             if step > full + d:
@@ -158,11 +163,15 @@
                 arrived(tokens_of(origin), asend, arecv.at[d, step - 1])
             if step < full + d:
                 tokens(d, step, origin)
-            hand(origin)
-        if step == LEG:
-            second_leg()
-        fill(FILL1)
+            hand(2 * step - 1 + d if step <= full else ring - 1, origin)
+            if step > 1:
+                first_leg(-step if d == 0 else step)
+        if step > 1:
+            fill(FILL1)
         if step == Q1:
+            with jax.named_scope("next"):
+                handed(0, t)
+                handed(2, at(2))
             straight(0)
 
     tile = 256
@@ -187,10 +196,10 @@
         return describe(part.at[j, d, part_of(b)], rsbuf.at[j, d, s], rsend.at[j, d], rrecv.at[j, d, s],
                         sub=lax.rem(x + (1 if d == 0 else subs - 1), subs))
 
-    def rs_step(group, s):
-        with jax.named_scope(f"reduce{s}"):
+    def rs_step(group):
+        with jax.named_scope(f"reduce{group[-1][1]}"):
             ready = None
-            for j in group:
+            for j, s in group:
                 for d in (0, 1):
                     b = lax.rem(x - 2 - s + 2 * subs, subs) if d == 0 else lax.rem(x + 2 + s, subs)
                     rs_copy(j, d, s).wait_recv()
@@ -205,32 +214,39 @@
                     part[j, d, part_of(b), :] = total
                     rs_copy(j, d, s).wait_send()
                     if ready is not None:
-                        rs_copy(*ready, s + 1).start()
-                    ready = (j, d)
+                        rs_copy(*ready).start()
+                    ready = j, d, s + 1
             if ready is not None:
-                rs_copy(*ready, s + 1).start()
+                rs_copy(*ready).start()
 
     with jax.named_scope("mate"):
-        arrived(acts.at[pl.ds(0, ring * toks)], apsend, aprecv)
+        for step in range(1, full + 1):
+            handed(2 * step - 1, at(-2 * step))
+            if step > 1:
+                handed(2 * step, at(2 * step))
+        handed(ring - 1, at(ring))
+    second_leg()
+    fill(FILL2)
 
     for k in range(pairs):
         product(k, sendq, k * cap)
+    for s in range(AHEAD):
+        rs_step([(k, s) for k in range(pairs)])
     with jax.named_scope("leg2"):
         arrived(kvsend.at[pl.ds(1, tp - 1)], k2send, k2recv)
-    product(pairs, kvraw, 0)
     fill(FILL)
     straight(far)
-    group = list(range(pairs + 1))
+    product(pairs, kvraw, 0)
     for s in range(subs - 1):
-        rs_step(group, s)
-    back = range(heads)
-    for i in back:
-        remote(res.at[i], sraw.at[i], ss_send, ss_recv, tp=at(dist[i // cap]))
+        rs_step([(k, s + AHEAD) for k in range(pairs) if s + AHEAD < subs - 1] + [(pairs, s)])
+        if s + AHEAD == subs - 2:
+            for i in range(heads):
+                remote(res.at[i], sraw.at[i], ss_send, ss_recv, tp=at(dist[i // cap]))
     for i, r in enumerate(routes(tp, t, heads, tgt_ref, src_ref, False)):
         gat[i] = r
     table = pltpu.make_async_copy(gat, gat_ref, ld.at[0])
     table.start()
-    for j in group:
+    for j in range(pairs + 1):
         for d in (0, 1):
             rs_copy(j, d, subs - 2).wait_send()
 
@@ -300,7 +316,9 @@
             dma((4,)),
             dma,
             dma((2, full + 1)),
-            *[dma] * 8,
+            dma,
+            dma((ring,)),
+            *[dma] * 6,
             dma((heads // 2 + 1, 2)),
             dma((heads // 2 + 1, 2, subs - 1)),
             dma,

time: 191 us -> 186 us (0.974)
  Pallas kernels: 189 us -> 184 us
    pallas_call x1, Pallas kernels: 186 us -> 181 us  [per_device(): pl.pallas_call(functools.partial(exchange, tp, subs), out_shape=(pltpu.VM...]
where the time goes in v4:
time: 186 us
  Pallas kernels  184 us (99%)
    pallas_call x1, Pallas kernels, per_device(): pl.pallas_call(functools.partial(exchange, tp, subs), out_shape=(pltpu.VM...  181 us

profile of v4, /device:TPU:513, one launch (start us, length us, event | category | flops | bytes accessed | tf_op | source)
XLA Modules:
  0.0 185.5 jit_solution(3824797540608236975)
XLA Ops:
  0.6 181.0 %exchange.1 = (bf16[8,2048,128]{2,1,0:T(8,128)(2,1)S(1)}, bf16[2,2048,128]{2,1,0:T(8,128)(2,1)S(1)}, bf16[8,128,128]{2,1,0:T(8,128)(2,1)S(1)}, bf16[2,128,128]{2,1,0:T(8,128)(2,1)S(1)}, s32[8]{0:T(128)}) custom-call(s32[128]{0:T(128)} %src_ref.1, s32[128]{0:T(128)} %tgt_ref.1, s32[16]{0:T(128)} %kvt_ref.1, bf16[64,2048]{1,0:T(8,128)(2,1)} %acts_ref.1, ...), custom_call_target="tpu_custom_call" | custom-call | tf_op jit(solution)/shard_map/exchange/pallas_call | solution.py:294
  181.6 0.0 copy-start
  181.6 0.6 copy-done
  182.3 3.2 %place.1 = (bf16[2048,1024]{1,0:T(8,128)(2,1)}, bf16[2048,256]{1,0:T(8,128)(2,1)}, bf16[128,1280]{1,0:T(8,128)(2,1)}) custom-call(s32[8]{0:T(128)S(1)} %copy-done, bf16[8,2048,128]{2,1,0:T(8,128)(2,1)S(1)} %get-tuple-element.9.qraw, bf16[2,2048,128]{2,1,0:T(8,128)(2,1)S(1)} %get-tuple-element.10.kvraw, bf16[8,128,128]{2,1,0:T(8,128)(2,1)S(1)} %get-tuple-element.11.sraw, ...), custom_call_target="tpu_custom_call" | custom-call | tf_op jit(solution)/shard_map/place/pallas_call | solution.py:331
Async XLA Ops:
  181.6 0.6 copy-start

commit v5 on v4

--- a/solution.py
+++ b/solution.py
@@ -48,9 +48,9 @@
     return pl.multiple_of(index * size, size)
 
 
-def exchange(tp, subs, src_ref, tgt_ref, kvt_ref, acts_ref, q_ref, kv_ref, qraw, kvraw, sraw, kvres, gat_ref,
-             gat, acts, qv, sendq, kvown, kvbuf, kvsend, part, rsbuf, res, ld, asend, arecv, apsend, aprecv,
-             k1send, k1recv, k2send, k2recv, qsend, qrecv, rsend, rrecv, ss_send, ss_recv):
+def exchange(tp, subs, src_ref, tgt_ref, kvt_ref, acts_ref, q_ref, kv_ref, qraw, kvraw, sraw, kvres, gat,
+             acts, qv, sendq, kvown, kvbuf, kvsend, relay, part, rsbuf, res, ld, asend, arecv, apsend, aprecv,
+             k1send, k1recv, k2send, k2recv, qsend, qrecv, rsend, rrecv, ss_send, ss_recv, hsend, hrecv):
     t, x = lax.axis_index("tp"), lax.axis_index("sub")
     core, y = lax.rem(t, 2), t // 2
     ring = tp // 2
@@ -143,7 +143,10 @@
 
     def straight(k):
         for i in range(k * cap, (k + 1) * cap):
-            remote(sendq.at[i], qraw.at[i], qsend, qrecv, tp=at(dist[k]))
+            whole = pl.ds(0, rows - (piece if k == far and i == detour else 0))
+            remote(sendq.at[i, whole], qraw.at[i, whole], qsend, qrecv, tp=at(dist[k]))
+
+    detour, end = (far + 1) * cap - 1, pl.ds(rows - piece, piece)
 
     def second_leg():
         with jax.named_scope("leg1"):
@@ -225,6 +228,7 @@
             if step > 1:
                 handed(2 * step, at(2 * step))
         handed(ring - 1, at(ring))
+    remote(sendq.at[detour, end], relay, qsend, hrecv, tp=at(-2))
     second_leg()
     fill(FILL2)
 
@@ -234,6 +238,8 @@
         rs_step([(k, s) for k in range(pairs)])
     with jax.named_scope("leg2"):
         arrived(kvsend.at[pl.ds(1, tp - 1)], k2send, k2recv)
+    arrived(relay, hsend, hrecv)
+    remote(relay, qraw.at[detour, end], hsend, qrecv, tp=at(2 - dist[far]))
     fill(FILL)
     straight(far)
     product(pairs, kvraw, 0)
@@ -244,17 +250,14 @@
                 remote(res.at[i], sraw.at[i], ss_send, ss_recv, tp=at(dist[i // cap]))
     for i, r in enumerate(routes(tp, t, heads, tgt_ref, src_ref, False)):
         gat[i] = r
-    table = pltpu.make_async_copy(gat, gat_ref, ld.at[0])
-    table.start()
     for j in range(pairs + 1):
         for d in (0, 1):
             rs_copy(j, d, subs - 2).wait_send()
 
-    table.wait()
     with jax.named_scope("sent"):
         for src, sem in ((acts.at[pl.ds(0, (2 * full + 1) * toks)], asend), (acts.at[pl.ds(0, ring * toks)], apsend),
                          (kvbuf.at[pl.ds(1, ring - 1)], k1send), (kvsend.at[pl.ds(1, tp - 1)], k2send),
-                         (sendq, qsend), (res, ss_send)):
+                         (sendq, qsend), (res, ss_send), (relay, hsend)):
             describe(src, src, sem, sem, tp=t).wait_send()
     with jax.named_scope("heads"):
         arrived(qraw, qsend, qrecv)
@@ -298,18 +301,18 @@
             pltpu.VMEM((2, *wide), BF16),
             pltpu.VMEM((heads, block, HD), BF16),
             pltpu.VMEM((2, block, HD), BF16),
-            jax.ShapeDtypeStruct((heads,), jnp.int32),
+            pltpu.SMEM((heads,), jnp.int32),
         ),
         in_specs=[smem, smem, smem, anyp, anyp, anyp],
-        out_specs=(vmem, vmem, vmem, vmem, anyp),
+        out_specs=(vmem, vmem, vmem, vmem, smem),
         scratch_shapes=[
-            pltpu.SMEM((heads,), jnp.int32),
             pltpu.VMEM((tokens, depth), BF16),
             pltpu.VMEM((heads, *wide), BF16),
             pltpu.VMEM((heads, *wide), BF16),
             pltpu.VMEM(wide, BF16),
             pltpu.VMEM((ring, rows // ring, HD), BF16),
             pltpu.VMEM((tp, rows // ring, HD), BF16),
+            pltpu.VMEM((rows // ring, HD), BF16),
             pltpu.VMEM((heads // 2 + 1, 2, tokens, HD), F32),
             pltpu.VMEM((heads // 2 + 1, 2, subs - 1, block, HD), F32),
             pltpu.VMEM((heads, block, HD), BF16),
@@ -321,6 +324,8 @@
             *[dma] * 6,
             dma((heads // 2 + 1, 2)),
             dma((heads // 2 + 1, 2, subs - 1)),
+            dma,
+            dma,
             dma,
             dma,
         ],
@@ -340,7 +345,7 @@
         scratch_shapes=[dma((4, heads))],
         compiler_params=pltpu.CompilerParams(vmem_limit_bytes=2**20),
         name="place",
-    )(gat, *(pltpu.with_memory_space_constraint(a, pltpu.VMEM) for a in raw))
+    )(pltpu.with_memory_space_constraint(gat, pltpu.SMEM), *(pltpu.with_memory_space_constraint(a, pltpu.VMEM) for a in raw))
 
 
 def solution(mesh):

time: 186 us -> 182 us (0.978)
  Pallas kernels: 184 us -> 181 us
    pallas_call x1, Pallas kernels: 181 us -> 178 us  [per_device(): pl.pallas_call(functools.partial(exchange, tp, subs), out_shape=(pltpu.VM...]
where the time goes in v5:
time: 182 us
  Pallas kernels  181 us (99%)
    pallas_call x1, Pallas kernels, per_device(): pl.pallas_call(functools.partial(exchange, tp, subs), out_shape=(pltpu.VM...  178 us

profile of v5, /device:TPU:513, one launch (start us, length us, event | category | flops | bytes accessed | tf_op | source)
XLA Modules:
  0.0 181.6 jit_solution(14893485508148077914)
XLA Ops:
  0.6 178.3 %exchange.1 = (bf16[8,2048,128]{2,1,0:T(8,128)(2,1)S(1)}, bf16[2,2048,128]{2,1,0:T(8,128)(2,1)S(1)}, bf16[8,128,128]{2,1,0:T(8,128)(2,1)S(1)}, bf16[2,128,128]{2,1,0:T(8,128)(2,1)S(1)}, s32[8]{0:T(128)S(4)}) custom-call(s32[128]{0:T(128)} %src_ref.1, s32[128]{0:T(128)} %tgt_ref.1, s32[16]{0:T(128)} %kvt_ref.1, bf16[64,2048]{1,0:T(8,128)(2,1)} %acts_ref.1, ...), custom_call_target="tpu_custom_call" | custom-call | tf_op jit(solution)/shard_map/exchange/pallas_call | solution.py:297
  178.9 2.7 %place.1 = (bf16[2048,1024]{1,0:T(8,128)(2,1)}, bf16[2048,256]{1,0:T(8,128)(2,1)}, bf16[128,1280]{1,0:T(8,128)(2,1)}) custom-call(s32[8]{0:T(128)S(4)} %get-tuple-element.8.gat, bf16[8,2048,128]{2,1,0:T(8,128)(2,1)S(1)} %get-tuple-element.9.qraw, bf16[2,2048,128]{2,1,0:T(8,128)(2,1)S(1)} %get-tuple-element.10.kvraw, ...), custom_call_target="tpu_custom_call" | custom-call | tf_op jit(solution)/shard_map/place/pallas_call | solution.py:336

commit v6 on v5

--- a/solution.py
+++ b/solution.py
@@ -95,14 +95,19 @@
     for copy in loads:
         copy.start()
     barrier = pltpu.get_barrier_semaphore()
-    for peer in (at(2), at(-2), mate):
+    for peer in (at(2), at(-2)):
         pl.semaphore_signal(barrier, inc=1, device_id={"tp": peer})
+
+    @pl.when(core == 1)
+    def _():
+        pl.semaphore_signal(barrier, inc=1, device_id={"tp": mate})
+
     for d in (1, subs - 1):
         pl.semaphore_signal(barrier, inc=1, device_id={"sub": lax.rem(x + d, subs)})
     for copy in loads[:3]:
         copy.wait()
     with jax.named_scope("barrier"):
-        pl.semaphore_wait(barrier, 5)
+        pl.semaphore_wait(barrier, 5 - core)
 
     def tokens(d, step, origin):
         remote(tokens_of(origin), tokens_of(origin), asend, arecv.at[d, step], tp=at(2 - 4 * d))
@@ -115,7 +120,11 @@
 
     tokens(0, 0, t)
     tokens(1, 0, t)
-    hand(0, t)
+    @pl.when(core == 0)
+    def _():
+        hand(0, t)
+
+    waiting = []
     def first_leg(d):
         remote(kvown.at[rows_of(chip(d))], kvbuf.at[y], k1send, k1recv, tp=at(2 * d))
 
@@ -166,14 +175,29 @@
                 arrived(tokens_of(origin), asend, arecv.at[d, step - 1])
             if step < full + d:
                 tokens(d, step, origin)
-            hand(2 * step - 1 + d if step <= full else ring - 1, origin)
+            turn = 2 * step - 1 + d if step <= full else ring - 1, origin
+            if step <= Q1:
+                waiting.append(turn)
+            else:
+                hand(*turn)
             if step > 1:
                 first_leg(-step if d == 0 else step)
         if step > 1:
             fill(FILL1)
         if step == Q1:
             with jax.named_scope("next"):
-                handed(0, t)
+                @pl.when(core == 1)
+                def _():
+                    handed(0, t)
+                    hand(0, t)
+
+                for turn in waiting:
+                    hand(*turn)
+
+                @pl.when(core == 0)
+                def _():
+                    handed(0, t)
+
                 handed(2, at(2))
             straight(0)
 

time: 182 us -> 178 us (0.978)
  Pallas kernels: 181 us -> 177 us
    pallas_call x1, Pallas kernels: 178 us -> 174 us  [per_device(): pl.pallas_call(functools.partial(exchange, tp, subs), out_shape=(pltpu.VM...]
where the time goes in v6:
time: 178 us; the launch traced here: 177 us
  Pallas kernels  177 us (99%)
    pallas_call x1, Pallas kernels, per_device(): pl.pallas_call(functools.partial(exchange, tp, subs), out_shape=(pltpu.VM...  174 us

profile of v6, /device:TPU:513, one launch (start us, length us, event | category | flops | bytes accessed | tf_op | source)
XLA Modules:
  0.0 177.4 jit_solution(11194081606078023020)
XLA Ops:
  0.6 174.0 %exchange.1 = (bf16[8,2048,128]{2,1,0:T(8,128)(2,1)S(1)}, bf16[2,2048,128]{2,1,0:T(8,128)(2,1)S(1)}, bf16[8,128,128]{2,1,0:T(8,128)(2,1)S(1)}, bf16[2,128,128]{2,1,0:T(8,128)(2,1)S(1)}, s32[8]{0:T(128)S(4)}) custom-call(s32[128]{0:T(128)} %src_ref.1, s32[128]{0:T(128)} %tgt_ref.1, s32[16]{0:T(128)} %kvt_ref.1, bf16[64,2048]{1,0:T(8,128)(2,1)} %acts_ref.1, ...), custom_call_target="tpu_custom_call" | custom-call | tf_op jit(solution)/shard_map/exchange/pallas_call | solution.py:321
  174.7 2.7 %place.1 = (bf16[2048,1024]{1,0:T(8,128)(2,1)}, bf16[2048,256]{1,0:T(8,128)(2,1)}, bf16[128,1280]{1,0:T(8,128)(2,1)}) custom-call(s32[8]{0:T(128)S(4)} %get-tuple-element.8.gat, bf16[8,2048,128]{2,1,0:T(8,128)(2,1)S(1)} %get-tuple-element.9.qraw, bf16[2,2048,128]{2,1,0:T(8,128)(2,1)S(1)} %get-tuple-element.10.kvraw, ...), custom_call_target="tpu_custom_call" | custom-call | tf_op jit(solution)/shard_map/place/pallas_call | solution.py:360
